TPU v7x, 32 devices: a whole 2x2x4 slice. The times are simulated.
32 devices in a mesh: shard: 8 (over z, x), rep: 4 (over y, core).
Axes of the slice: x: 2, y: 2, z: 4, core: 2. Of those that a mesh axis runs over, the one named last changes fastest.
Arguments:
- activations: bfloat16 [4, 2048, 2048], P(None, ('shard', 'rep')), may hold values from -6 to 6
- value_grad: bfloat16 [4, 2048, 512], P(None, ('shard', 'rep')), may hold values from -6 to 6
- norm_gain: bfloat16 [2048], P('shard'), may hold values from 0.25 to 4.5
- value_weight: bfloat16 [2048, 512], P('shard'), may hold values from -0.125 to 0.125
Outputs:
- input_grad: bfloat16 [4, 2048, 2048], P(None, ('shard', 'rep'))
- weight_update: float32 [2048, 512], P('shard')
All inputs are finite; a program needn't handle non-finite values.
Results may differ from a plain program's by a relative error of at most 0.0029.
Values may be sent and summed in bfloat16 or wider, within the bound.
No kernel may reach another device: no remote copies, remote signals or barrier semaphores. Data moves between devices by JAX's collectives and lax.ppermute only.
A program may use at most 64 MiB of HBM per device.

v0:
```python
import jax
import jax.numpy as jnp
from jax import lax
from jax.sharding import PartitionSpec as P


def on_device(activations, value_grad, norm_gain, value_weight):
    gain_all, weight_all = (
        lax.all_gather(norm_gain, "shard", axis=0, tiled=True),
        lax.all_gather(value_weight, "shard", axis=0, tiled=True),
    )
    gain = gain_all.astype(jnp.float32)
    width = activations.shape[2]
    columns = value_grad.shape[2]

    def one_batch(total, inputs):
        block, cotangent = inputs
        values = block.astype(jnp.float32)
        rstd = lax.rsqrt(jnp.mean(values * values, axis=-1, keepdims=True) + 1e-05)
        normed = (values * rstd * gain).astype(jnp.bfloat16)
        total = total + lax.dot_general(
            normed, cotangent, (((0,), (0,)), ((), ())), preferred_element_type=jnp.float32
        )
        normed_grad = jnp.dot(cotangent, weight_all.T, preferred_element_type=jnp.float32)
        scaled = normed_grad * gain
        inner = jnp.mean(scaled * values, axis=-1, keepdims=True)
        result = (rstd * scaled - values * rstd * rstd * rstd * inner).astype(jnp.bfloat16)
        return (total, result)

    start = jnp.zeros((width, columns), jnp.float32)
    grad_full, input_grad = lax.scan(one_batch, start, (activations, value_grad))
    partial_rows = lax.psum_scatter(grad_full, "shard", scatter_dimension=0, tiled=True)
    summed = lax.psum(partial_rows, "rep")
    squares = lax.psum(jnp.sum(summed * summed), "shard")
    factor = 1.0 / jnp.maximum(1.0, jnp.sqrt(squares / (width * columns)))
    return (input_grad, summed * factor)


def solution(mesh):
    in_specs = (
        P(None, ("shard", "rep"), None),
        P(None, ("shard", "rep"), None),
        P("shard"),
        P("shard", None),
    )
    out_specs = (P(None, ("shard", "rep"), None), P("shard", None))
    return jax.shard_map(
        on_device, mesh=mesh, in_specs=in_specs, out_specs=out_specs, check_vma=False
    )
```

profile of v0, /device:TPU:0, one launch (start us, length us, event | category | flops | bytes accessed | tf_op | source)
XLA Modules:
  0.0 250.8 jit_solution(5175639290680449490)
XLA Ops:
  7.2 0.7 all-gather.3.cloned.1.call-update
  7.9 0.0 reduce-scatter.2.cloned.1.call-start
  8.0 0.7 reshape.34
  8.6 22.4 %all-gather = bf16[8,1,256]{2,1,0:T(2,128)(2,1)S(1)} all-gather(bf16[1,1,256]{2,1,0:T(2,128)(2,1)S(1)} %reshape.34), channel_id=1, replica_groups=mesh['shard'=8,'rep'=4] {'shard'}, dimensions={0}, use_global_device_ids=true | all-gather | bytes 4608 | tf_op jit(solution)/shard_map/all_gather | solution.py:9
  31.0 31.0 %all-gather.3.cloned.1.call-done = bf16[2048,512]{1,0:T(8,128)(2,1)} async-done(((bf16[256,512]{1,0:T(8,128)(2,1)}), bf16[2048,512]{1,0:T(8,128)(2,1)}) %all-gather.3.cloned.1.call-update) | async-done | bytes 2097168 | tf_op jit(solution)/shard_map/all_gather | solution.py:10
  62.0 33.5 %while.13 = (s32[]{:T(128)}, f32[2048,512]{1,0:T(8,128)}, bf16[4,64,2048]{2,1,0:T(8,128)(2,1)S(1)}, bf16[4,64,2048]{2,1,0:T(8,128)(2,1)}, f32[2048]{0:T(1024)S(1...) while((s32[]{:T(128)}, f32[2048,512]{1,0:T(8,128)}, ...), condition=%wide.region_3.4_spmd.clone, body=%wide.region_0.3_spmd.clone.sunk | while | flops 272891968 | bytes 12735858 | solution.py:31
  62.0 2.5 fusion.34
  64.5 1.2 fusion.35
  65.6 3.7 %select_add_fusion.2 = f32[2048,512]{1,0:T(8,128)} fusion(f32[2048,512]{1,0:T(8,128)} %get-tuple-element.148, pred[]{:T(512)S(6)} %compare.3, f32[2048]{0:T(1024)S(1)} %get-tuple-element.160, f32[64]{0:T(128)S(1)} %get-tuple-element.135, bf16[4,64,2048]{2,1,0:T(8,128)(2,1)} %get-tuple-element.159, s32[]{:T(128)S(6)} %copy.10, ...), kind=kOutput, calls=%fused_computation.clone.1 | convolution fusion | flops 136839168 | bytes 8726272 | tf_op jit(solution)/shard_map/while/body/eval_jaxpr/dot_general | solution.py:21
  69.3 2.5 fusion.34
  71.8 1.2 fusion.35
  73.0 5.1 %select_add_fusion.2 = f32[2048,512]{1,0:T(8,128)} fusion(f32[2048,512]{1,0:T(8,128)} %get-tuple-element.148, pred[]{:T(512)S(6)} %compare.3, f32[2048]{0:T(1024)S(1)} %get-tuple-element.160, f32[64]{0:T(128)S(1)} %get-tuple-element.135, bf16[4,64,2048]{2,1,0:T(8,128)(2,1)} %get-tuple-element.159, s32[]{:T(128)S(6)} %copy.10, ...), kind=kOutput, calls=%fused_computation.clone.1 | convolution fusion | flops 136839168 | bytes 8726272 | tf_op jit(solution)/shard_map/while/body/eval_jaxpr/dot_general | solution.py:21
  78.0 2.5 fusion.34
  80.5 1.2 fusion.35
  81.7 5.1 %select_add_fusion.2 = f32[2048,512]{1,0:T(8,128)} fusion(f32[2048,512]{1,0:T(8,128)} %get-tuple-element.148, pred[]{:T(512)S(6)} %compare.3, f32[2048]{0:T(1024)S(1)} %get-tuple-element.160, f32[64]{0:T(128)S(1)} %get-tuple-element.135, bf16[4,64,2048]{2,1,0:T(8,128)(2,1)} %get-tuple-element.159, s32[]{:T(128)S(6)} %copy.10, ...), kind=kOutput, calls=%fused_computation.clone.1 | convolution fusion | flops 136839168 | bytes 8726272 | tf_op jit(solution)/shard_map/while/body/eval_jaxpr/dot_general | solution.py:21
  86.7 2.5 fusion.34
  89.2 1.2 fusion.35
  90.4 5.1 %select_add_fusion.2 = f32[2048,512]{1,0:T(8,128)} fusion(f32[2048,512]{1,0:T(8,128)} %get-tuple-element.148, pred[]{:T(512)S(6)} %compare.3, f32[2048]{0:T(1024)S(1)} %get-tuple-element.160, f32[64]{0:T(128)S(1)} %get-tuple-element.135, bf16[4,64,2048]{2,1,0:T(8,128)(2,1)} %get-tuple-element.159, s32[]{:T(128)S(6)} %copy.10, ...), kind=kOutput, calls=%fused_computation.clone.1 | convolution fusion | flops 136839168 | bytes 8726272 | tf_op jit(solution)/shard_map/while/body/eval_jaxpr/dot_general | solution.py:21
  95.5 0.0 all-reduce.2.cloned.1.call-start
  95.5 87.0 %reduce-scatter.2.cloned.1.call-done = f32[256,512]{1,0:T(8,128)} async-done(((f32[2048,512]{1,0:T(8,128)}), f32[256,512]{1,0:T(8,128)}) %reduce-scatter.2.cloned.1.call-update) | async-done | bytes 524304 | tf_op jit(solution)/shard_map/reduce_scatter | solution.py:32
  182.5 35.4 %all-reduce.2.cloned.1.call-done = f32[256,512]{1,0:T(8,128)} async-done(((f32[256,512]{1,0:T(8,128)}), f32[256,512]{1,0:T(8,128)}) %all-reduce.2.cloned.1.call-update) | async-done | bytes 524304 | tf_op jit(solution)/shard_map/psum | solution.py:33
  217.9 1.8 multiply_reduce_fusion
  219.7 22.0 %psum.15 = f32[]{:T(128)} all-reduce(f32[]{:T(128)} %multiply_reduce_fusion), channel_id=1, replica_groups=mesh['shard'=8,'rep'=4] {'shard'}, use_global_device_ids=true, to_apply=%region_7.8 | all-reduce | flops 1 | bytes 8 | tf_op jit(solution)/shard_map/psum | solution.py:34
  242.4 1.9 broadcast_multiply_fusion.1
  (12 shorter events, 0.1 us)
Async XLA Ops:
  7.2 54.8 %all-gather.3.cloned.1.call-start = ((), (), s32[]{:S(2)}) async-start(), calls=%async_computation.1 | async-start | bytes 2359296 | tf_op jit(solution)/shard_map/all_gather | solution.py:10
  7.9 174.6 %reduce-scatter.2.cloned.1.call-start = ((), (), s32[]{:S(2)}) async-start(), calls=%async_computation.2 | async-start | bytes 4718592 | tf_op jit(solution)/shard_map/reduce_scatter | solution.py:32
  95.5 148.8 %copy-start = (bf16[4,64,2048]{2,1,0:T(8,128)(2,1)}, bf16[4,64,2048]{2,1,0:T(8,128)(2,1)S(1)}, u32[]{:S(2)}) copy-start(bf16[4,64,2048]{2,1,0:T(8,128)(2,1)S(1)} %get-tuple-element.38) | copy-start | bytes 3145732
  95.5 122.4 %all-reduce.2.cloned.1.call-start = ((), (), s32[]{:S(2)}) async-start(), calls=%async_computation.3 | async-start | bytes 1048576 | tf_op jit(solution)/shard_map/psum | solution.py:33
Sparse Core Ops, SparseCore 0:
  10.1 51.8 all-gather.2
  95.6 86.8 reduce-scatter.1
  184.8 33.0 all-reduce.1
where the time goes:
time: 251 us
  waiting for transfers between devices  154 us (61%)
  blocking collectives  44.3 us (18%)
  matrix products  28.8 us (11%)
  between operations  14.5 us (6%)
  other arithmetic  8.3 us (3%)
    reduce_scatter x1, waiting for transfers between devices, on_device(): lax.psum_scatter(grad_full, 'shard', scatter_dimension=0, tiled=True)  87 us
    psum x1, waiting for transfers between devices, on_device(): summed = lax.psum(partial_rows, 'rep')  35.4 us
    all_gather x1, waiting for transfers between devices, on_device(): lax.all_gather(value_weight, 'shard', axis=0, tiled=True)  31 us
    all_gather x1, blocking collectives, on_device(): lax.all_gather(norm_gain, 'shard', axis=0, tiled=True)  22.4 us
    psum x1, blocking collectives, on_device(): squares = lax.psum(jnp.sum(summed * summed), 'shard')  22 us
    dot_general x4, matrix products, one_batch(): lax.dot_general(normed, cotangent, (((0,), (0,)), ((), ())), preferred_el...  18.9 us
    dot_general x4, matrix products, one_batch(): jnp.dot(cotangent, weight_all.T, preferred_element_type=jnp.float32)  9.84 us
  transfers between devices with their start and end apart: 3, of which 3 were waited for; matrix products, arithmetic and copies ran while one was open for 0% of the time, Pallas kernels for 0%

commit v1 on v0

--- a/solution.py
+++ b/solution.py
@@ -30,7 +30,8 @@
     start = jnp.zeros((width, columns), jnp.float32)
     grad_full, input_grad = lax.scan(one_batch, start, (activations, value_grad))
     partial_rows = lax.psum_scatter(grad_full, "shard", scatter_dimension=0, tiled=True)
-    summed = lax.psum(partial_rows, "rep")
+    pieces = lax.all_gather(partial_rows, "rep")
+    summed = jnp.sum(pieces, axis=0)
     squares = lax.psum(jnp.sum(summed * summed), "shard")
     factor = 1.0 / jnp.maximum(1.0, jnp.sqrt(squares / (width * columns)))
     return (input_grad, summed * factor)

time: 251 us -> 239 us (0.952)
  waiting for transfers between devices: 154 us -> 142 us
    psum x1 -> x0, waiting for transfers between devices: 35.4 us -> none  [on_device(): summed = lax.psum(partial_rows, 'rep')]
    all_gather x0 -> x1, waiting for transfers between devices: none -> 23.8 us  [on_device(): pieces = lax.all_gather(partial_rows, 'rep')]
where the time goes in v1:
time: 239 us
  waiting for transfers between devices  142 us (59%)
  blocking collectives  44.3 us (19%)
  matrix products  28.8 us (12%)
  between operations  14.5 us (6%)
  other arithmetic  8.08 us (3%)
    reduce_scatter x1, waiting for transfers between devices, on_device(): lax.psum_scatter(grad_full, 'shard', scatter_dimension=0, tiled=True)  87 us
    all_gather x1, waiting for transfers between devices, on_device(): lax.all_gather(value_weight, 'shard', axis=0, tiled=True)  31 us
    all_gather x1, waiting for transfers between devices, on_device(): pieces = lax.all_gather(partial_rows, 'rep')  23.8 us
    all_gather x1, blocking collectives, on_device(): lax.all_gather(norm_gain, 'shard', axis=0, tiled=True)  22.4 us
    psum x1, blocking collectives, on_device(): squares = lax.psum(jnp.sum(summed * summed), 'shard')  22 us
    dot_general x4, matrix products, one_batch(): lax.dot_general(normed, cotangent, (((0,), (0,)), ((), ())), preferred_el...  18.9 us
    dot_general x4, matrix products, one_batch(): jnp.dot(cotangent, weight_all.T, preferred_element_type=jnp.float32)  9.84 us
  transfers between devices with their start and end apart: 3, of which 3 were waited for; matrix products, arithmetic and copies ran while one was open for 0% of the time, Pallas kernels for 0%

profile of v1, /device:TPU:0, one launch (start us, length us, event | category | flops | bytes accessed | tf_op | source)
XLA Modules:
  0.0 239.0 jit_solution(4784809478658846876)
XLA Ops:
  7.2 0.7 all-gather.5.cloned.1.call-update
  8.0 0.7 reshape.35
  8.6 22.4 %all-gather.1 = bf16[8,1,256]{2,1,0:T(2,128)(2,1)S(1)} all-gather(bf16[1,1,256]{2,1,0:T(2,128)(2,1)S(1)} %reshape.35), channel_id=1, replica_groups=mesh['shard'=8,'rep'=4] {'shard'}, dimensions={0}, use_global_device_ids=true | all-gather | bytes 4608 | tf_op jit(solution)/shard_map/all_gather | solution.py:9
  31.0 31.0 %all-gather.5.cloned.1.call-done = bf16[2048,512]{1,0:T(8,128)(2,1)} async-done(((bf16[256,512]{1,0:T(8,128)(2,1)}), bf16[2048,512]{1,0:T(8,128)(2,1)}) %all-gather.5.cloned.1.call-update) | async-done | bytes 2097168 | tf_op jit(solution)/shard_map/all_gather | solution.py:10
  62.0 33.5 %while.13 = (s32[]{:T(128)}, f32[2048,512]{1,0:T(8,128)}, bf16[4,64,2048]{2,1,0:T(8,128)(2,1)S(1)}, bf16[4,64,2048]{2,1,0:T(8,128)(2,1)}, f32[2048]{0:T(1024)S(1...) while((s32[]{:T(128)}, f32[2048,512]{1,0:T(8,128)}, ...), condition=%wide.region_3.4_spmd.clone, body=%wide.region_0.3_spmd.clone.sunk | while | flops 272891968 | bytes 12735858 | solution.py:31
  62.0 2.5 %fusion.34 = (f32[64]{0:T(128)S(1)}, f32[64]{0:T(128)S(1)}, f32[64,2048]{1,0:T(8,128)S(1)}) fusion(bf16[4,64,2048]{2,1,0:T(8,128)(2,1)} %get-tuple-element.159, s32[]{:T(128)S(6)} %copy.10, f32[2048]{0:T(1024)S(1)} %get-tuple-element.160, bf16[2048,512]{1,0:T(8,128)(2,1)} %get-tuple-element.162, bf16[4,64,512]{2,1,0:T(8,128)(2,1)} %get-tuple-element.161), kind=kOutput, calls=%fused_computation.13.clone.1 | convolution fusion | flops 135004032 | bytes 2958848 | tf_op jit(solution)/shard_map/while/body/eval_jaxpr/dot_general | solution.py:24
  64.5 1.2 fusion.35
  65.6 3.7 %select_add_fusion.2 = f32[2048,512]{1,0:T(8,128)} fusion(f32[2048,512]{1,0:T(8,128)} %get-tuple-element.148, pred[]{:T(512)S(6)} %compare.3, f32[2048]{0:T(1024)S(1)} %get-tuple-element.160, f32[64]{0:T(128)S(1)} %get-tuple-element.135, bf16[4,64,2048]{2,1,0:T(8,128)(2,1)} %get-tuple-element.159, s32[]{:T(128)S(6)} %copy.10, ...), kind=kOutput, calls=%fused_computation.clone.1 | convolution fusion | flops 136839168 | bytes 8726272 | tf_op jit(solution)/shard_map/while/body/eval_jaxpr/dot_general | solution.py:21
  69.3 2.5 %fusion.34 = (f32[64]{0:T(128)S(1)}, f32[64]{0:T(128)S(1)}, f32[64,2048]{1,0:T(8,128)S(1)}) fusion(bf16[4,64,2048]{2,1,0:T(8,128)(2,1)} %get-tuple-element.159, s32[]{:T(128)S(6)} %copy.10, f32[2048]{0:T(1024)S(1)} %get-tuple-element.160, bf16[2048,512]{1,0:T(8,128)(2,1)} %get-tuple-element.162, bf16[4,64,512]{2,1,0:T(8,128)(2,1)} %get-tuple-element.161), kind=kOutput, calls=%fused_computation.13.clone.1 | convolution fusion | flops 135004032 | bytes 2958848 | tf_op jit(solution)/shard_map/while/body/eval_jaxpr/dot_general | solution.py:24
  71.8 1.2 fusion.35
  73.0 5.1 %select_add_fusion.2 = f32[2048,512]{1,0:T(8,128)} fusion(f32[2048,512]{1,0:T(8,128)} %get-tuple-element.148, pred[]{:T(512)S(6)} %compare.3, f32[2048]{0:T(1024)S(1)} %get-tuple-element.160, f32[64]{0:T(128)S(1)} %get-tuple-element.135, bf16[4,64,2048]{2,1,0:T(8,128)(2,1)} %get-tuple-element.159, s32[]{:T(128)S(6)} %copy.10, ...), kind=kOutput, calls=%fused_computation.clone.1 | convolution fusion | flops 136839168 | bytes 8726272 | tf_op jit(solution)/shard_map/while/body/eval_jaxpr/dot_general | solution.py:21
  78.0 2.5 %fusion.34 = (f32[64]{0:T(128)S(1)}, f32[64]{0:T(128)S(1)}, f32[64,2048]{1,0:T(8,128)S(1)}) fusion(bf16[4,64,2048]{2,1,0:T(8,128)(2,1)} %get-tuple-element.159, s32[]{:T(128)S(6)} %copy.10, f32[2048]{0:T(1024)S(1)} %get-tuple-element.160, bf16[2048,512]{1,0:T(8,128)(2,1)} %get-tuple-element.162, bf16[4,64,512]{2,1,0:T(8,128)(2,1)} %get-tuple-element.161), kind=kOutput, calls=%fused_computation.13.clone.1 | convolution fusion | flops 135004032 | bytes 2958848 | tf_op jit(solution)/shard_map/while/body/eval_jaxpr/dot_general | solution.py:24
  80.5 1.2 fusion.35
  81.7 5.1 %select_add_fusion.2 = f32[2048,512]{1,0:T(8,128)} fusion(f32[2048,512]{1,0:T(8,128)} %get-tuple-element.148, pred[]{:T(512)S(6)} %compare.3, f32[2048]{0:T(1024)S(1)} %get-tuple-element.160, f32[64]{0:T(128)S(1)} %get-tuple-element.135, bf16[4,64,2048]{2,1,0:T(8,128)(2,1)} %get-tuple-element.159, s32[]{:T(128)S(6)} %copy.10, ...), kind=kOutput, calls=%fused_computation.clone.1 | convolution fusion | flops 136839168 | bytes 8726272 | tf_op jit(solution)/shard_map/while/body/eval_jaxpr/dot_general | solution.py:21
  86.7 2.5 %fusion.34 = (f32[64]{0:T(128)S(1)}, f32[64]{0:T(128)S(1)}, f32[64,2048]{1,0:T(8,128)S(1)}) fusion(bf16[4,64,2048]{2,1,0:T(8,128)(2,1)} %get-tuple-element.159, s32[]{:T(128)S(6)} %copy.10, f32[2048]{0:T(1024)S(1)} %get-tuple-element.160, bf16[2048,512]{1,0:T(8,128)(2,1)} %get-tuple-element.162, bf16[4,64,512]{2,1,0:T(8,128)(2,1)} %get-tuple-element.161), kind=kOutput, calls=%fused_computation.13.clone.1 | convolution fusion | flops 135004032 | bytes 2958848 | tf_op jit(solution)/shard_map/while/body/eval_jaxpr/dot_general | solution.py:24
  89.2 1.2 fusion.35
  90.4 5.1 %select_add_fusion.2 = f32[2048,512]{1,0:T(8,128)} fusion(f32[2048,512]{1,0:T(8,128)} %get-tuple-element.148, pred[]{:T(512)S(6)} %compare.3, f32[2048]{0:T(1024)S(1)} %get-tuple-element.160, f32[64]{0:T(128)S(1)} %get-tuple-element.135, bf16[4,64,2048]{2,1,0:T(8,128)(2,1)} %get-tuple-element.159, s32[]{:T(128)S(6)} %copy.10, ...), kind=kOutput, calls=%fused_computation.clone.1 | convolution fusion | flops 136839168 | bytes 8726272 | tf_op jit(solution)/shard_map/while/body/eval_jaxpr/dot_general | solution.py:21
  95.5 0.0 all-gather.7.cloned.1.call-start
  95.5 87.0 %reduce-scatter.2.cloned.1.call-done = f32[256,512]{1,0:T(8,128)} async-done(((f32[2048,512]{1,0:T(8,128)}), f32[256,512]{1,0:T(8,128)}) %reduce-scatter.2.cloned.1.call-update) | async-done | bytes 524304 | tf_op jit(solution)/shard_map/reduce_scatter | solution.py:32
  182.5 23.8 %all-gather.7.cloned.1.call-done = f32[1024,512]{1,0:T(8,128)} async-done(((f32[256,512]{1,0:T(8,128)}), f32[1024,512]{1,0:T(8,128)}) %all-gather.7.cloned.1.call-update) | async-done | bytes 2097168 | tf_op jit(solution)/shard_map/all_gather | solution.py:33
  206.3 1.9 reduce_sum.36
  208.2 0.7 multiply_reduce_fusion
  208.9 22.0 %psum.7 = f32[]{:T(128)} all-reduce(f32[]{:T(128)} %multiply_reduce_fusion), channel_id=1, replica_groups=mesh['shard'=8,'rep'=4] {'shard'}, use_global_device_ids=true, to_apply=%region_7.8 | all-reduce | flops 1 | bytes 8 | tf_op jit(solution)/shard_map/psum | solution.py:35
  231.6 0.8 broadcast_multiply_fusion.1
  (13 shorter events, 0.1 us)
Async XLA Ops:
  7.2 54.8 %all-gather.5.cloned.1.call-start = ((), (), s32[]{:S(2)}) async-start(), calls=%async_computation.1 | async-start | bytes 2359296 | tf_op jit(solution)/shard_map/all_gather | solution.py:10
  7.9 174.6 %reduce-scatter.2.cloned.1.call-start = ((), (), s32[]{:S(2)}) async-start(), calls=%async_computation.2 | async-start | bytes 4718592 | tf_op jit(solution)/shard_map/reduce_scatter | solution.py:32
  95.5 137.0 %copy-start = (bf16[4,64,2048]{2,1,0:T(8,128)(2,1)}, bf16[4,64,2048]{2,1,0:T(8,128)(2,1)S(1)}, u32[]{:S(2)}) copy-start(bf16[4,64,2048]{2,1,0:T(8,128)(2,1)S(1)} %get-tuple-element.38) | copy-start | bytes 3145732
  95.5 110.8 %all-gather.7.cloned.1.call-start = ((), (), s32[]{:S(2)}) async-start(), calls=%async_computation.3 | async-start | bytes 2621440 | tf_op jit(solution)/shard_map/all_gather | solution.py:33
Sparse Core Ops, SparseCore 0:
  10.1 51.8 all-gather.4
  95.6 86.8 reduce-scatter.1
  184.1 22.1 all-gather.6
